TPU v7x, 512 devices: a whole 4x4x16 slice. The times are simulated.
512 devices in a mesh: task: 4 (over z_hi, core), seq: 16 (over x, y), dp: 8 (over z_lo).
Axes of the slice: x: 4, y: 4, z: 16 (z_hi: 2, z_lo: 8; z = z_hi * 8 + z_lo), core: 2. Of those that a mesh axis runs over, the one named last changes fastest.
Arguments:
- enc_grads: bfloat16 [4, 8, 2048, 4096], P('task', 'dp', 'seq'), may hold values from -12 to 12
- hidden: bfloat16 [8, 2048, 4096], P('dp', 'seq', 'task'), may hold values from -900 to 900
- final_gain: float32 [4096], replicated, may hold values from 0.1 to 1.9
- attn_out: bfloat16 [8, 2048, 4096], P('dp', 'seq', 'task'), may hold values from -6 to 6
- qkv: bfloat16 [8, 2048, 64, 192], P('dp', None, ('task', 'seq')), may hold values from -48 to 48
- out_weight: bfloat16 [4096, 4096], P('task', ('seq', 'dp')), may hold values from -0.09375 to 0.09375
- doc_lengths: int32 [8], P('dp'), may hold values from 512 to 2048
Outputs:
- resid_grad: bfloat16 [8, 2048, 4096], P('dp', 'seq', 'task')
- qkv_grad: bfloat16 [8, 2048, 64, 192], P('dp', None, ('task', 'seq'))
- weight_grad: float32 [4096, 4096], P('task', ('seq', 'dp'))
Inputs may be any that keep to these rules, and one draw needn't show every extreme that they name: `doc_lengths`: positions at or after a document's length are padding and are never attended to as keys.
All inputs are finite; a program needn't handle non-finite values.
Results may differ from a plain program's by a relative error of at most 0.02.
Values may be sent and summed in bfloat16 or wider, within the bound.
No kernel may reach another device: no remote copies, remote signals or barrier semaphores. Data moves between devices by JAX's collectives and lax.ppermute only.
A program may use at most 64 MiB of HBM per device.

v0:
```python
import jax
import jax.numpy as jnp
from jax import lax
from jax.sharding import PartitionSpec as P

eps_norm = 1e-06


def split_up(shard, dim, peers):
    lengths = shard.shape
    pieces = shard.reshape(*lengths[:dim], peers, lengths[dim] // peers, *lengths[dim + 1 :])
    return jnp.moveaxis(pieces, dim, 0)


def sent_and_summed(shard, axis, dim):
    pieces = split_up(shard, dim, lax.axis_size(axis))
    arrived = lax.all_to_all(pieces, axis, split_axis=0, concat_axis=0, tiled=True)
    return arrived.astype(jnp.float32).sum(axis=0)


def copy_for_each(shard, axis):
    copies = jnp.broadcast_to(shard, (lax.axis_size(axis), *shard.shape))
    return lax.all_to_all(copies, axis, split_axis=0, concat_axis=0, tiled=True)


def over_copies(shard, axis):
    everything = copy_for_each(shard, axis)
    return jnp.sum(everything, axis=0)


def packed_total(arrays, axis):
    ends = [0]
    for a in arrays:
        ends.append(ends[-1] + a.size)
    running = over_copies(jnp.concatenate([a.ravel() for a in arrays]), axis)
    return tuple((running[b:e].reshape(a.shape) for a, b, e in zip(arrays, ends, ends[1:])))


def joined_along(pieces, dim):
    lengths = list(pieces.shape[1:])
    lengths[dim] *= pieces.shape[0]
    return jnp.moveaxis(pieces, 0, dim).reshape(lengths)


def gather_directly(shard, axis, dim):
    return joined_along(copy_for_each(shard, axis), dim)


def on_device(enc_grads, hidden, final_gain, attn_out, qkv, out_weight, doc_lengths):
    feature_cols = enc_grads.shape[3]
    task_count = lax.axis_size("task")
    task_pos = lax.axis_index("task")
    share_cols = feature_cols // task_count
    partial_terms = enc_grads[0, 0].astype(jnp.float32)
    summed = sent_and_summed(partial_terms.astype(jnp.bfloat16), "task", 1)
    rows_part = hidden[0].astype(jnp.float32)
    gain_part = lax.dynamic_slice_in_dim(final_gain, task_pos * share_cols, share_cols, 0)
    squares, cross_sum = packed_total(
        (jnp.sum(rows_part * rows_part, axis=-1), jnp.sum(gain_part * summed * rows_part, axis=-1)),
        "task",
    )
    scale_inv = lax.rsqrt(squares / feature_cols + eps_norm)[:, None]
    cross_mean = cross_sum[:, None] * scale_inv / feature_cols
    resid_part = (scale_inv * (gain_part * summed - rows_part * scale_inv * cross_mean)).astype(
        jnp.bfloat16
    )
    resid_full = gather_directly(resid_part, "task", 1)
    weight_slab = gather_directly(out_weight, "dp", 1)
    resid_slice = resid_full
    head_grad = lax.dot_general(
        resid_slice,
        lax.all_gather(weight_slab, "seq", axis=1, tiled=True),
        (((1,), (1,)), ((), ())),
        preferred_element_type=jnp.float32,
    )
    head_grad = head_grad.astype(jnp.bfloat16)
    saved_tok = attn_out[0]
    out_heads, saved_heads = (
        lax.all_to_all(head_grad, "seq", split_axis=1, concat_axis=0, tiled=True),
        lax.all_to_all(saved_tok, "seq", split_axis=1, concat_axis=0, tiled=True),
    )
    resid_cols = lax.all_to_all(resid_full, "seq", split_axis=1, concat_axis=0, tiled=True)
    resid_slice = resid_cols
    grad_block = lax.dot_general(
        lax.all_gather(saved_tok, "seq", axis=0, tiled=True),
        resid_slice,
        (((0,), (0,)), ((), ())),
        preferred_element_type=jnp.float32,
    )
    seq_len = qkv.shape[1]
    weight_grad = sent_and_summed(grad_block.astype(jnp.bfloat16), "dp", 1)
    head_size = qkv.shape[3] // 3
    doc_length = doc_lengths[0]
    key_valid = (jnp.arange(seq_len, dtype=jnp.int32) < doc_length)[None, :]
    block_rows = min(512, seq_len)
    block_count = seq_len // block_rows
    query = qkv[0, :, 0, :head_size]
    key_rows = qkv[0, :, 0, head_size : 2 * head_size]
    value_rows = qkv[0, :, 0, 2 * head_size :]
    delta_rows = jnp.sum(out_heads.astype(jnp.float32) * saved_heads.astype(jnp.float32), axis=-1)

    def block_step(state_pair, block_index):
        key_acc, value_acc = state_pair
        row_start = block_index * block_rows
        query_blk = lax.dynamic_slice_in_dim(query, row_start, block_rows, 0)
        upstream_blk = lax.dynamic_slice_in_dim(out_heads, row_start, block_rows, 0)
        delta_blk = lax.dynamic_slice_in_dim(delta_rows, row_start, block_rows, 0)
        scores = lax.dot_general(
            query_blk, key_rows, (((1,), (1,)), ((), ())), preferred_element_type=jnp.float32
        )
        scores = jnp.where(key_valid, scores, -1e30)
        row_max = jnp.max(scores, axis=-1, keepdims=True)
        expo_terms = jnp.exp(scores - row_max)
        prob_rows = expo_terms / jnp.sum(expo_terms, axis=-1, keepdims=True)
        prob_bf16 = prob_rows.astype(jnp.bfloat16)
        value_acc = value_acc + lax.dot_general(
            prob_bf16, upstream_blk, (((0,), (0,)), ((), ())), preferred_element_type=jnp.float32
        )
        dprob_rows = lax.dot_general(
            upstream_blk, value_rows, (((1,), (1,)), ((), ())), preferred_element_type=jnp.float32
        )
        dscore_rows = (prob_rows * (dprob_rows - delta_blk[:, None])).astype(jnp.bfloat16)
        dquery = jnp.dot(dscore_rows, key_rows, preferred_element_type=jnp.float32).astype(
            jnp.bfloat16
        )
        key_acc = key_acc + lax.dot_general(
            dscore_rows, query_blk, (((0,), (0,)), ((), ())), preferred_element_type=jnp.float32
        )
        return ((key_acc, value_acc), dquery)

    zero_pair = (
        jnp.zeros((seq_len, head_size), jnp.float32),
        jnp.zeros((seq_len, head_size), jnp.float32),
    )
    (key_acc, value_acc), dq_blocks = lax.scan(
        block_step, zero_pair, jnp.arange(block_count, dtype=jnp.int32)
    )
    dquery_all = dq_blocks.reshape(seq_len, head_size)
    head_grads = [
        jnp.concatenate(
            [dquery_all, key_acc.astype(jnp.bfloat16), value_acc.astype(jnp.bfloat16)], axis=-1
        )
    ]
    qkv_grad = jnp.stack(head_grads, axis=1)[None]
    return (resid_part[None], qkv_grad, weight_grad)


def solution(mesh):
    return jax.shard_map(
        on_device,
        mesh=mesh,
        in_specs=(
            P("task", "dp", "seq", None),
            P("dp", "seq", "task"),
            P(),
            P("dp", "seq", "task"),
            P("dp", None, ("task", "seq"), None),
            P("task", ("seq", "dp")),
            P("dp"),
        ),
        out_specs=(
            P("dp", "seq", "task"),
            P("dp", None, ("task", "seq"), None),
            P("task", ("seq", "dp")),
        ),
        check_vma=False,
    )
```

profile of v0, /device:TPU:8, one launch (start us, length us, event | category | flops | bytes accessed | tf_op | source)
XLA Modules:
  0.0 326.9 jit_solution(1640961790241758674)
XLA Ops:
  8.8 41.2 %all_to_all.77 = bf16[8,1024,32]{1,2,0:T(8,128)(2,1)} all-to-all(bf16[8,1024,32]{1,2,0:T(8,128)(2,1)S(1)} %broadcast_in_dim.42), channel_id=1, replica_groups=mesh['task'=4,'seq'=16,'dp'=8] {'dp'}, dimensions={0} | all-to-all | bytes 1048576 | tf_op jit(solution)/shard_map/all_to_all | solution.py:23
  50.0 1.7 copy.68
  53.1 7.6 %all-to-all-start = ((bf16[4,128,1024]{2,1,0:T(8,128)(2,1)}), bf16[4,128,1024]{2,1,0:T(8,128)(2,1)S(1)}, u32[]{:S(2)}, u32[]{:S(2)}) async-start(bf16[4,128,1024]{2,1,0:T(8,128)(2,1)} %copy.69), calls=%async_computation | async-start | bytes 2097152 | tf_op jit(solution)/shard_map/all_to_all | solution.py:17
  61.3 44.1 %all-to-all-done = bf16[4,128,1024]{2,1,0:T(8,128)(2,1)S(1)} async-done(((bf16[4,128,1024]{2,1,0:T(8,128)(2,1)}), bf16[4,128,1024]{2,1,0:T(8,128)(2,1)S(1)}, u32[]{:S(2)}, u32[]{:S(2)}) %all-to-all-start) | async-done | bytes 1048608 | tf_op jit(solution)/shard_map/all_to_all | solution.py:17
  105.8 14.8 %all_to_all.78 = f32[4,1,256]{2,1,0:T(1,128)S(1)} all-to-all(f32[4,1,256]{2,1,0:T(1,128)S(1)} %broadcast_in_dim.39), channel_id=1, replica_groups=mesh['task'=4,'seq'=16,'dp'=8] {'task'}, dimensions={0} | all-to-all | bytes 8192 | tf_op jit(solution)/shard_map/all_to_all | solution.py:23
  121.2 30.5 %all_to_all.79 = bf16[4,128,1024]{1,2,0:T(8,128)(2,1)S(1)} all-to-all(bf16[4,128,1024]{1,2,0:T(8,128)(2,1)S(1)} %broadcast_in_dim.41), channel_id=1, replica_groups=mesh['task'=4,'seq'=16,'dp'=8] {'task'}, dimensions={0} | all-to-all | bytes 2097152 | tf_op jit(solution)/shard_map/all_to_all | solution.py:23
  151.8 30.4 %all_to_all.80 = bf16[128,16,256]{0,2,1:T(8,128)(2,1)S(1)} all-to-all(bf16[128,16,256]{0,2,1:T(8,128)(2,1)S(1)} %bitcast.93), channel_id=1, replica_groups=mesh['task'=4,'seq'=16,'dp'=8] {'seq'}, dimensions={1} | all-to-all | bytes 2097152 | tf_op jit(solution)/shard_map/all_to_all | solution.py:82
  183.5 4.6 %fusion.19 = bf16[256,1024]{1,0:T(8,128)(2,1)} fusion(bf16[2048,256]{1,0:T(8,128)(2,1)} %bitcast.100, bf16[1,2048,1024]{2,1,0:T(8,128)(2,1)} %all-gather.6.cloned.1.call-done), kind=kOutput, calls=%fused_computation.25 | convolution fusion | flops 1074003968 | bytes 5767168 | tf_op jit(solution)/shard_map/dot_general | solution.py:84
  188.1 25.5 %all-to-all-start.7 = ((bf16[8,1024,32]{1,2,0:T(8,128)(2,1)}), bf16[8,1024,32]{1,2,0:T(8,128)(2,1)S(1)}, u32[]{:S(2)}, u32[]{:S(2)}) async-start(bf16[8,1024,32]{1,2,0:T(8,128)(2,1)} %bitcast.25), calls=%async_computation.7 | async-start | bytes 1048576 | tf_op jit(solution)/shard_map/all_to_all | solution.py:17
  214.5 4.7 %convolution_convert_fusion.1 = bf16[128,1024]{1,0:T(8,128)(2,1)S(1)} fusion(bf16[128,4096]{0,1:T(8,128)(2,1)S(1)} %bitcast.94, bf16[1024,4096]{0,1:T(8,128)(2,1)} %all-gather.4.cloned.1.call-done), kind=kOutput, calls=%fused_computation.26 | convolution fusion | flops 1073872896 | bytes 9699328 | tf_op jit(solution)/shard_map/dot_general | solution.py:70
  220.0 21.6 %all-to-all-done.7 = bf16[8,1024,32]{1,2,0:T(8,128)(2,1)S(1)} async-done(((bf16[8,1024,32]{1,2,0:T(8,128)(2,1)}), bf16[8,1024,32]{1,2,0:T(8,128)(2,1)S(1)}, u32[]{:S(2)}, u32[]{:S(2)}) %all-to-all-start.7) | async-done | bytes 524320 | tf_op jit(solution)/shard_map/all_to_all | solution.py:17
  241.6 5.1 %all-to-all-start.4 = ((bf16[128,16,64]{0,2,1:T(8,128)(2,1)}), bf16[128,16,64]{0,2,1:T(8,128)(2,1)S(1)}, u32[]{:S(2)}, u32[]{:S(2)}) async-start(bf16[128,16,64]{0,2,1:T(8,128)(2,1)} %bitcast.10), calls=%async_computation.4 | async-start | bytes 524288 | tf_op jit(solution)/shard_map/all_to_all | solution.py:79
  249.4 4.6 %all-to-all-done.4 = bf16[128,16,64]{0,2,1:T(8,128)(2,1)S(1)} async-done(((bf16[128,16,64]{0,2,1:T(8,128)(2,1)}), bf16[128,16,64]{0,2,1:T(8,128)(2,1)S(1)}, u32[]{:S(2)}, u32[]{:S(2)}) %all-to-all-start.4) | async-done | bytes 262176 | tf_op jit(solution)/shard_map/all_to_all | solution.py:79
  254.1 5.1 %all-to-all-start.5 = ((bf16[128,16,64]{0,2,1:T(8,128)(2,1)}), bf16[128,16,64]{0,2,1:T(8,128)(2,1)S(1)}, u32[]{:S(2)}, u32[]{:S(2)}) async-start(bf16[128,16,64]{0,2,1:T(8,128)(2,1)} %bitcast.14), calls=%async_computation.5 | async-start | bytes 524288 | tf_op jit(solution)/shard_map/all_to_all | solution.py:80
  261.1 5.0 %all-to-all-done.5 = bf16[128,16,64]{0,2,1:T(8,128)(2,1)S(1)} async-done(((bf16[128,16,64]{0,2,1:T(8,128)(2,1)}), bf16[128,16,64]{0,2,1:T(8,128)(2,1)S(1)}, u32[]{:S(2)}, u32[]{:S(2)}) %all-to-all-start.5) | async-done | bytes 262176 | tf_op jit(solution)/shard_map/all_to_all | solution.py:80
  266.2 50.8 %while.15 = (s32[]{:T(128)}, f32[2048,64]{0,1:T(8,128)S(1)}, f32[2048,64]{0,1:T(8,128)}, bf16[4,512,64]{1,2,0:T(8,128)(2,1)}, s32[4]{0:T(128)S(1)}, /*index=5*/b...) while((s32[]{:T(128)}, f32[2048,64]{0,1:T(8,128)S(1)}, ...), condition=%wide.region_8.9_spmd.clone, body=%wide.region_5.8_spmd.clone.sunk | while | flops 687375360 | bytes 65895284 | solution.py:135
  269.0 1.9 copy-done
  271.8 3.5 %convolution_add_fusion.5 = f32[2048,64]{0,1:T(8,128)S(1)} fusion(f32[2048,64]{0,1:T(8,128)S(1)} %copy-done.5, pred[]{:T(512)S(6)} %compare.3, bf16[2048,64]{1,0:T(8,128)(2,1)S(1)} %get-tuple-element.298, s32[]{:T(128)S(6)} %select_n.35, f32[512,2048]{1,0:T(8,128)} %copy-done, f32[512]{0:T(512)S(1)} %fusion.65, f32[512]{0:T(512)S(1)} %get-tuple-element.260, ...), kind=kOutput, calls=%fused_computation.6.clone.1 | convolution fusion | flops 138674176 | bytes 5380101 | tf_op jit(solution)/shard_map/while/body/eval_jaxpr/dot_general | solution.py:116
  275.3 1.6 multiply_convert_fusion.2
  277.5 1.4 fusion.66
  281.7 1.9 copy-done
  284.5 3.5 %convolution_add_fusion.5 = f32[2048,64]{0,1:T(8,128)S(1)} fusion(f32[2048,64]{0,1:T(8,128)S(1)} %copy-done.5, pred[]{:T(512)S(6)} %compare.3, bf16[2048,64]{1,0:T(8,128)(2,1)S(1)} %get-tuple-element.298, s32[]{:T(128)S(6)} %select_n.35, f32[512,2048]{1,0:T(8,128)} %copy-done, f32[512]{0:T(512)S(1)} %fusion.65, f32[512]{0:T(512)S(1)} %get-tuple-element.260, ...), kind=kOutput, calls=%fused_computation.6.clone.1 | convolution fusion | flops 138674176 | bytes 5380101 | tf_op jit(solution)/shard_map/while/body/eval_jaxpr/dot_general | solution.py:116
  288.0 1.6 multiply_convert_fusion.2
  290.2 1.4 fusion.66
  294.4 1.9 copy-done
  297.1 3.5 %convolution_add_fusion.5 = f32[2048,64]{0,1:T(8,128)S(1)} fusion(f32[2048,64]{0,1:T(8,128)S(1)} %copy-done.5, pred[]{:T(512)S(6)} %compare.3, bf16[2048,64]{1,0:T(8,128)(2,1)S(1)} %get-tuple-element.298, s32[]{:T(128)S(6)} %select_n.35, f32[512,2048]{1,0:T(8,128)} %copy-done, f32[512]{0:T(512)S(1)} %fusion.65, f32[512]{0:T(512)S(1)} %get-tuple-element.260, ...), kind=kOutput, calls=%fused_computation.6.clone.1 | convolution fusion | flops 138674176 | bytes 5380101 | tf_op jit(solution)/shard_map/while/body/eval_jaxpr/dot_general | solution.py:116
  300.7 1.6 multiply_convert_fusion.2
  302.9 1.4 fusion.66
  307.0 1.9 copy-done
  309.8 3.5 %convolution_add_fusion.5 = f32[2048,64]{0,1:T(8,128)S(1)} fusion(f32[2048,64]{0,1:T(8,128)S(1)} %copy-done.5, pred[]{:T(512)S(6)} %compare.3, bf16[2048,64]{1,0:T(8,128)(2,1)S(1)} %get-tuple-element.298, s32[]{:T(128)S(6)} %select_n.35, f32[512,2048]{1,0:T(8,128)} %copy-done, f32[512]{0:T(512)S(1)} %fusion.65, f32[512]{0:T(512)S(1)} %get-tuple-element.260, ...), kind=kOutput, calls=%fused_computation.6.clone.1 | convolution fusion | flops 138674176 | bytes 5380101 | tf_op jit(solution)/shard_map/while/body/eval_jaxpr/dot_general | solution.py:116
  313.4 1.6 multiply_convert_fusion.2
  315.6 1.4 fusion.66
  (101 shorter events, 29.7 us)
Async XLA Ops:
  7.2 176.3 %all-gather.6.cloned.1.call-start = ((), (), s32[]{:S(2)}) async-start(), calls=%async_computation.9 | async-start | bytes 4456448 | tf_op jit(solution)/shard_map/all_gather | solution.py:85
  7.9 206.6 %all-gather.4.cloned.1.call-start = ((), (), s32[]{:S(2)}) async-start(), calls=%async_computation.8 | async-start | bytes 8912896 | tf_op jit(solution)/shard_map/all_gather | solution.py:72
  50.0 55.6 %copy-start.2 = (bf16[1,128,1024]{2,1,0:T(8,128)(2,1)S(1)}, bf16[1,128,1024]{2,1,0:T(8,128)(2,1)}, u32[]{:S(2)}) copy-start(bf16[1,128,1024]{2,1,0:T(8,128)(2,1)} %param.10) | copy-start | bytes 786436
  53.1 52.4 %all-to-all-start = ((bf16[4,128,1024]{2,1,0:T(8,128)(2,1)}), bf16[4,128,1024]{2,1,0:T(8,128)(2,1)S(1)}, u32[]{:S(2)}, u32[]{:S(2)}) async-start(bf16[4,128,1024]{2,1,0:T(8,128)(2,1)} %copy.69), calls=%async_computation | async-start | bytes 2097152 | tf_op jit(solution)/shard_map/all_to_all | solution.py:17
  183.5 30.1 %copy-start.3 = (bf16[1,128,1024]{2,1,0:T(8,128)(2,1)S(1)}, bf16[1,128,1024]{2,1,0:T(8,128)(2,1)}, u32[]{:S(2)}) copy-start(bf16[1,128,1024]{2,1,0:T(8,128)(2,1)} %param.12) | copy-start | bytes 786436
  188.1 53.5 %all-to-all-start.7 = ((bf16[8,1024,32]{1,2,0:T(8,128)(2,1)}), bf16[8,1024,32]{1,2,0:T(8,128)(2,1)S(1)}, u32[]{:S(2)}, u32[]{:S(2)}) async-start(bf16[8,1024,32]{1,2,0:T(8,128)(2,1)} %bitcast.25), calls=%async_computation.7 | async-start | bytes 1048576 | tf_op jit(solution)/shard_map/all_to_all | solution.py:17
  241.6 12.5 %all-to-all-start.4 = ((bf16[128,16,64]{0,2,1:T(8,128)(2,1)}), bf16[128,16,64]{0,2,1:T(8,128)(2,1)S(1)}, u32[]{:S(2)}, u32[]{:S(2)}) async-start(bf16[128,16,64]{0,2,1:T(8,128)(2,1)} %bitcast.10), calls=%async_computation.4 | async-start | bytes 524288 | tf_op jit(solution)/shard_map/all_to_all | solution.py:79
  254.1 12.1 %all-to-all-start.5 = ((bf16[128,16,64]{0,2,1:T(8,128)(2,1)}), bf16[128,16,64]{0,2,1:T(8,128)(2,1)S(1)}, u32[]{:S(2)}, u32[]{:S(2)}) async-start(bf16[128,16,64]{0,2,1:T(8,128)(2,1)} %bitcast.14), calls=%async_computation.5 | async-start | bytes 524288 | tf_op jit(solution)/shard_map/all_to_all | solution.py:80
  268.2 3.6 %copy-start.5 = (f32[2048,64]{0,1:T(8,128)S(1)}, f32[2048,64]{0,1:T(8,128)}, u32[]{:S(2)}) copy-start(f32[2048,64]{0,1:T(8,128)} %get-tuple-element.278) | copy-start | bytes 1572868 | tf_op jit(solution)/shard_map/while
  269.0 1.9 copy-start
  271.7 3.6 %copy-start.1 = (f32[512,2048]{1,0:T(8,128)S(1)}, f32[512,2048]{1,0:T(8,128)}, u32[]{:S(2)}) copy-start(f32[512,2048]{1,0:T(8,128)} %copy-done) | copy-start | bytes 12582916 | tf_op jit(solution)/shard_map/while
  271.8 3.6 %copy-start.4 = (bf16[2048,64]{1,0:T(8,128)(2,1)S(1)}, bf16[2048,64]{1,0:T(8,128)(2,1)}, u32[]{:S(2)}) copy-start(bf16[2048,64]{1,0:T(8,128)(2,1)} %get-tuple-element.299) | copy-start | bytes 786436 | tf_op jit(solution)/shard_map/while
  275.2 1.7 copy-start.6
  280.9 3.6 %copy-start.5 = (f32[2048,64]{0,1:T(8,128)S(1)}, f32[2048,64]{0,1:T(8,128)}, u32[]{:S(2)}) copy-start(f32[2048,64]{0,1:T(8,128)} %get-tuple-element.278) | copy-start | bytes 1572868 | tf_op jit(solution)/shard_map/while
  281.7 1.9 copy-start
  284.4 3.6 %copy-start.1 = (f32[512,2048]{1,0:T(8,128)S(1)}, f32[512,2048]{1,0:T(8,128)}, u32[]{:S(2)}) copy-start(f32[512,2048]{1,0:T(8,128)} %copy-done) | copy-start | bytes 12582916 | tf_op jit(solution)/shard_map/while
  284.5 3.6 %copy-start.4 = (bf16[2048,64]{1,0:T(8,128)(2,1)S(1)}, bf16[2048,64]{1,0:T(8,128)(2,1)}, u32[]{:S(2)}) copy-start(bf16[2048,64]{1,0:T(8,128)(2,1)} %get-tuple-element.299) | copy-start | bytes 786436 | tf_op jit(solution)/shard_map/while
  287.9 1.7 copy-start.6
  293.6 3.6 %copy-start.5 = (f32[2048,64]{0,1:T(8,128)S(1)}, f32[2048,64]{0,1:T(8,128)}, u32[]{:S(2)}) copy-start(f32[2048,64]{0,1:T(8,128)} %get-tuple-element.278) | copy-start | bytes 1572868 | tf_op jit(solution)/shard_map/while
  294.4 1.9 copy-start
  297.1 3.6 %copy-start.1 = (f32[512,2048]{1,0:T(8,128)S(1)}, f32[512,2048]{1,0:T(8,128)}, u32[]{:S(2)}) copy-start(f32[512,2048]{1,0:T(8,128)} %copy-done) | copy-start | bytes 12582916 | tf_op jit(solution)/shard_map/while
  297.1 3.6 %copy-start.4 = (bf16[2048,64]{1,0:T(8,128)(2,1)S(1)}, bf16[2048,64]{1,0:T(8,128)(2,1)}, u32[]{:S(2)}) copy-start(bf16[2048,64]{1,0:T(8,128)(2,1)} %get-tuple-element.299) | copy-start | bytes 786436 | tf_op jit(solution)/shard_map/while
  300.6 1.7 copy-start.6
  306.2 3.6 %copy-start.5 = (f32[2048,64]{0,1:T(8,128)S(1)}, f32[2048,64]{0,1:T(8,128)}, u32[]{:S(2)}) copy-start(f32[2048,64]{0,1:T(8,128)} %get-tuple-element.278) | copy-start | bytes 1572868 | tf_op jit(solution)/shard_map/while
  307.0 1.9 copy-start
  309.8 3.6 %copy-start.1 = (f32[512,2048]{1,0:T(8,128)S(1)}, f32[512,2048]{1,0:T(8,128)}, u32[]{:S(2)}) copy-start(f32[512,2048]{1,0:T(8,128)} %copy-done) | copy-start | bytes 12582916 | tf_op jit(solution)/shard_map/while
  309.8 3.6 %copy-start.4 = (bf16[2048,64]{1,0:T(8,128)(2,1)S(1)}, bf16[2048,64]{1,0:T(8,128)(2,1)}, u32[]{:S(2)}) copy-start(bf16[2048,64]{1,0:T(8,128)(2,1)} %get-tuple-element.299) | copy-start | bytes 786436 | tf_op jit(solution)/shard_map/while
  313.3 1.7 copy-start.6
Sparse Core Ops, SparseCore 0:
  11.0 70.9 all-gather.5
  85.0 96.0 all-gather.3
where the time goes:
time: 328 us; the launch traced here: 327 us
  blocking collectives  117 us (36%)
  waiting for transfers between devices  76.1 us (23%)
  starting transfers between devices  43.4 us (13%)
  matrix products  40.7 us (12%)
  local copies, waits for them, and re-layouts  22.4 us (7%)
  between operations  14.2 us (4%)
  other arithmetic  10.4 us (3%)
    all_to_all x3, blocking collectives, copy_for_each(): return lax.all_to_all(copies, axis, split_axis=0, concat_axis=0, tiled=True)  86.5 us
    all_to_all x2, waiting for transfers between devices, sent_and_summed(): lax.all_to_all(pieces, axis, split_axis=0, concat_axis=0, tiled=True)  65.7 us
    all_to_all x2, starting transfers between devices, sent_and_summed(): lax.all_to_all(pieces, axis, split_axis=0, concat_axis=0, tiled=True)  33.1 us
    all_to_all x1, blocking collectives, on_device(): lax.all_to_all(resid_full, 'seq', split_axis=1, concat_axis=0, tiled=True)  30.4 us
    dot_general x4, matrix products, block_step(): lax.dot_general(prob_bf16, upstream_blk, (((0,), (0,)), ((), ())), prefer...  13.8 us
    while x40, local copies, waits for them, and re-layouts  7.78 us
  transfers between devices with their start and end apart: 6, of which 4 were waited for; matrix products, arithmetic and copies ran while one was open for 7% of the time, Pallas kernels for 0%

commit v1 on v0

--- a/solution.py
+++ b/solution.py
@@ -79,7 +79,10 @@
         lax.all_to_all(head_grad, "seq", split_axis=1, concat_axis=0, tiled=True),
         lax.all_to_all(saved_tok, "seq", split_axis=1, concat_axis=0, tiled=True),
     )
-    resid_cols = lax.all_to_all(resid_full, "seq", split_axis=1, concat_axis=0, tiled=True)
+    resid_cols = jnp.concatenate(
+        lax.all_to_all(jnp.stack(jnp.split(resid_full, lax.axis_size("seq"), axis=1)), "seq", 0, 0),
+        axis=0,
+    )
     resid_slice = resid_cols
     grad_block = lax.dot_general(
         lax.all_gather(saved_tok, "seq", axis=0, tiled=True),

time: 328 us -> 328 us (level)
  no operation moved by 1% of the time
where the time goes in v1:
time: 328 us; the launch traced here: 327 us
  blocking collectives  117 us (36%)
  waiting for transfers between devices  76.1 us (23%)
  starting transfers between devices  43.7 us (13%)
  matrix products  40.7 us (12%)
  local copies, waits for them, and re-layouts  22.6 us (7%)
  between operations  14.2 us (4%)
  other arithmetic  10.4 us (3%)
    all_to_all x3, blocking collectives, copy_for_each(): return lax.all_to_all(copies, axis, split_axis=0, concat_axis=0, tiled=True)  86.5 us
    all_to_all x2, waiting for transfers between devices, sent_and_summed(): lax.all_to_all(pieces, axis, split_axis=0, concat_axis=0, tiled=True)  65.7 us
    all_to_all x2, starting transfers between devices, sent_and_summed(): lax.all_to_all(pieces, axis, split_axis=0, concat_axis=0, tiled=True)  33.4 us
    all_to_all x1, blocking collectives, on_device(): lax.all_to_all(jnp.stack(jnp.split(resid_full, lax.axis_size('seq'), axis...  30.1 us
    dot_general x4, matrix products, block_step(): lax.dot_general(prob_bf16, upstream_blk, (((0,), (0,)), ((), ())), prefer...  13.8 us
    while x40, local copies, waits for them, and re-layouts  7.78 us
  transfers between devices with their start and end apart: 6, of which 4 were waited for; matrix products, arithmetic and copies ran while one was open for 7% of the time, Pallas kernels for 0%

profile of v1, /device:TPU:8, one launch (start us, length us, event | category | flops | bytes accessed | tf_op | source)
XLA Modules:
  0.0 327.2 jit_solution(11421948936153894410)
XLA Ops:
  8.8 41.2 %all_to_all.63 = bf16[8,1024,32]{1,2,0:T(8,128)(2,1)} all-to-all(bf16[8,1024,32]{1,2,0:T(8,128)(2,1)S(1)} %broadcast_in_dim.42), channel_id=1, replica_groups=mesh['task'=4,'seq'=16,'dp'=8] {'dp'}, dimensions={0} | all-to-all | bytes 1048576 | tf_op jit(solution)/shard_map/all_to_all | solution.py:23
  50.0 1.7 copy.67
  53.1 7.6 %all-to-all-start = ((bf16[4,128,1024]{2,1,0:T(8,128)(2,1)}), bf16[4,128,1024]{2,1,0:T(8,128)(2,1)S(1)}, u32[]{:S(2)}, u32[]{:S(2)}) async-start(bf16[4,128,1024]{2,1,0:T(8,128)(2,1)} %copy.68), calls=%async_computation | async-start | bytes 2097152 | tf_op jit(solution)/shard_map/all_to_all | solution.py:17
  61.3 44.1 %all-to-all-done = bf16[4,128,1024]{2,1,0:T(8,128)(2,1)S(1)} async-done(((bf16[4,128,1024]{2,1,0:T(8,128)(2,1)}), bf16[4,128,1024]{2,1,0:T(8,128)(2,1)S(1)}, u32[]{:S(2)}, u32[]{:S(2)}) %all-to-all-start) | async-done | bytes 1048608 | tf_op jit(solution)/shard_map/all_to_all | solution.py:17
  105.8 14.8 %all_to_all.64 = f32[4,1,256]{2,1,0:T(1,128)S(1)} all-to-all(f32[4,1,256]{2,1,0:T(1,128)S(1)} %broadcast_in_dim.39), channel_id=1, replica_groups=mesh['task'=4,'seq'=16,'dp'=8] {'task'}, dimensions={0} | all-to-all | bytes 8192 | tf_op jit(solution)/shard_map/all_to_all | solution.py:23
  121.2 30.5 %all_to_all.65 = bf16[4,128,1024]{1,2,0:T(8,128)(2,1)S(1)} all-to-all(bf16[4,128,1024]{1,2,0:T(8,128)(2,1)S(1)} %broadcast_in_dim.41), channel_id=1, replica_groups=mesh['task'=4,'seq'=16,'dp'=8] {'task'}, dimensions={0} | all-to-all | bytes 2097152 | tf_op jit(solution)/shard_map/all_to_all | solution.py:23
  152.0 30.1 %all_to_all.66 = bf16[16,128,256]{1,2,0:T(8,128)(2,1)S(1)} all-to-all(bf16[16,128,256]{1,2,0:T(8,128)(2,1)S(1)} %fusion.36), channel_id=1, replica_groups=mesh['task'=4,'seq'=16,'dp'=8] {'seq'}, dimensions={0} | all-to-all | bytes 2097152 | tf_op jit(solution)/shard_map/all_to_all | solution.py:83
  183.5 4.6 %fusion.19 = bf16[256,1024]{1,0:T(8,128)(2,1)} fusion(bf16[2048,256]{1,0:T(8,128)(2,1)} %bitcast.175, bf16[1,2048,1024]{2,1,0:T(8,128)(2,1)} %all-gather.6.cloned.1.call-done), kind=kOutput, calls=%fused_computation.25 | convolution fusion | flops 1074003968 | bytes 5767168 | tf_op jit(solution)/shard_map/dot_general | solution.py:87
  188.1 25.8 %all-to-all-start.7 = ((bf16[8,1024,32]{1,2,0:T(8,128)(2,1)}), bf16[8,1024,32]{1,2,0:T(8,128)(2,1)S(1)}, u32[]{:S(2)}, u32[]{:S(2)}) async-start(bf16[8,1024,32]{1,2,0:T(8,128)(2,1)} %bitcast.40), calls=%async_computation.7 | async-start | bytes 1048576 | tf_op jit(solution)/shard_map/all_to_all | solution.py:17
  214.8 4.7 %convolution_convert_fusion.1 = bf16[128,1024]{1,0:T(8,128)(2,1)S(1)} fusion(bf16[128,4096]{0,1:T(8,128)(2,1)S(1)} %bitcast.170, bf16[1024,4096]{0,1:T(8,128)(2,1)} %all-gather.4.cloned.1.call-done), kind=kOutput, calls=%fused_computation.26 | convolution fusion | flops 1073872896 | bytes 9699328 | tf_op jit(solution)/shard_map/dot_general | solution.py:70
  220.3 21.6 %all-to-all-done.7 = bf16[8,1024,32]{1,2,0:T(8,128)(2,1)S(1)} async-done(((bf16[8,1024,32]{1,2,0:T(8,128)(2,1)}), bf16[8,1024,32]{1,2,0:T(8,128)(2,1)S(1)}, u32[]{:S(2)}, u32[]{:S(2)}) %all-to-all-start.7) | async-done | bytes 524320 | tf_op jit(solution)/shard_map/all_to_all | solution.py:17
  241.9 5.1 %all-to-all-start.4 = ((bf16[128,16,64]{0,2,1:T(8,128)(2,1)}), bf16[128,16,64]{0,2,1:T(8,128)(2,1)S(1)}, u32[]{:S(2)}, u32[]{:S(2)}) async-start(bf16[128,16,64]{0,2,1:T(8,128)(2,1)} %bitcast.10), calls=%async_computation.4 | async-start | bytes 524288 | tf_op jit(solution)/shard_map/all_to_all | solution.py:79
  249.7 4.6 %all-to-all-done.4 = bf16[128,16,64]{0,2,1:T(8,128)(2,1)S(1)} async-done(((bf16[128,16,64]{0,2,1:T(8,128)(2,1)}), bf16[128,16,64]{0,2,1:T(8,128)(2,1)S(1)}, u32[]{:S(2)}, u32[]{:S(2)}) %all-to-all-start.4) | async-done | bytes 262176 | tf_op jit(solution)/shard_map/all_to_all | solution.py:79
  254.4 5.1 %all-to-all-start.5 = ((bf16[128,16,64]{0,2,1:T(8,128)(2,1)}), bf16[128,16,64]{0,2,1:T(8,128)(2,1)S(1)}, u32[]{:S(2)}, u32[]{:S(2)}) async-start(bf16[128,16,64]{0,2,1:T(8,128)(2,1)} %bitcast.14), calls=%async_computation.5 | async-start | bytes 524288 | tf_op jit(solution)/shard_map/all_to_all | solution.py:80
  261.4 5.0 %all-to-all-done.5 = bf16[128,16,64]{0,2,1:T(8,128)(2,1)S(1)} async-done(((bf16[128,16,64]{0,2,1:T(8,128)(2,1)}), bf16[128,16,64]{0,2,1:T(8,128)(2,1)S(1)}, u32[]{:S(2)}, u32[]{:S(2)}) %all-to-all-start.5) | async-done | bytes 262176 | tf_op jit(solution)/shard_map/all_to_all | solution.py:80
  266.5 50.7 %while.15 = (s32[]{:T(128)}, f32[2048,64]{0,1:T(8,128)S(1)}, f32[2048,64]{0,1:T(8,128)}, bf16[4,512,64]{1,2,0:T(8,128)(2,1)}, s32[4]{0:T(128)S(1)}, /*index=5*/b...) while((s32[]{:T(128)}, f32[2048,64]{0,1:T(8,128)S(1)}, ...), condition=%wide.region_8.9_spmd.clone, body=%wide.region_5.8_spmd.clone.sunk | while | flops 687375360 | bytes 65895284 | solution.py:138
  269.3 1.9 copy-done
  272.1 3.5 %convolution_add_fusion.5 = f32[2048,64]{0,1:T(8,128)S(1)} fusion(f32[2048,64]{0,1:T(8,128)S(1)} %copy-done.5, pred[]{:T(512)S(6)} %compare.3, bf16[2048,64]{1,0:T(8,128)(2,1)S(1)} %get-tuple-element.298, s32[]{:T(128)S(6)} %select_n.35, f32[512,2048]{1,0:T(8,128)} %copy-done, f32[512]{0:T(512)S(1)} %fusion.81, f32[512]{0:T(512)S(1)} %get-tuple-element.260, ...), kind=kOutput, calls=%fused_computation.6.clone.1 | convolution fusion | flops 138674176 | bytes 5380101 | tf_op jit(solution)/shard_map/while/body/eval_jaxpr/dot_general | solution.py:119
  275.6 1.6 multiply_convert_fusion.2
  277.8 1.4 fusion.82
  282.0 1.9 copy-done
  284.7 3.5 %convolution_add_fusion.5 = f32[2048,64]{0,1:T(8,128)S(1)} fusion(f32[2048,64]{0,1:T(8,128)S(1)} %copy-done.5, pred[]{:T(512)S(6)} %compare.3, bf16[2048,64]{1,0:T(8,128)(2,1)S(1)} %get-tuple-element.298, s32[]{:T(128)S(6)} %select_n.35, f32[512,2048]{1,0:T(8,128)} %copy-done, f32[512]{0:T(512)S(1)} %fusion.81, f32[512]{0:T(512)S(1)} %get-tuple-element.260, ...), kind=kOutput, calls=%fused_computation.6.clone.1 | convolution fusion | flops 138674176 | bytes 5380101 | tf_op jit(solution)/shard_map/while/body/eval_jaxpr/dot_general | solution.py:119
  288.3 1.6 multiply_convert_fusion.2
  290.5 1.4 fusion.82
  294.7 1.9 copy-done
  297.4 3.5 %convolution_add_fusion.5 = f32[2048,64]{0,1:T(8,128)S(1)} fusion(f32[2048,64]{0,1:T(8,128)S(1)} %copy-done.5, pred[]{:T(512)S(6)} %compare.3, bf16[2048,64]{1,0:T(8,128)(2,1)S(1)} %get-tuple-element.298, s32[]{:T(128)S(6)} %select_n.35, f32[512,2048]{1,0:T(8,128)} %copy-done, f32[512]{0:T(512)S(1)} %fusion.81, f32[512]{0:T(512)S(1)} %get-tuple-element.260, ...), kind=kOutput, calls=%fused_computation.6.clone.1 | convolution fusion | flops 138674176 | bytes 5380101 | tf_op jit(solution)/shard_map/while/body/eval_jaxpr/dot_general | solution.py:119
  301.0 1.6 multiply_convert_fusion.2
  303.2 1.4 fusion.82
  307.3 1.9 copy-done
  310.1 3.5 %convolution_add_fusion.5 = f32[2048,64]{0,1:T(8,128)S(1)} fusion(f32[2048,64]{0,1:T(8,128)S(1)} %copy-done.5, pred[]{:T(512)S(6)} %compare.3, bf16[2048,64]{1,0:T(8,128)(2,1)S(1)} %get-tuple-element.298, s32[]{:T(128)S(6)} %select_n.35, f32[512,2048]{1,0:T(8,128)} %copy-done, f32[512]{0:T(512)S(1)} %fusion.81, f32[512]{0:T(512)S(1)} %get-tuple-element.260, ...), kind=kOutput, calls=%fused_computation.6.clone.1 | convolution fusion | flops 138674176 | bytes 5380101 | tf_op jit(solution)/shard_map/while/body/eval_jaxpr/dot_general | solution.py:119
  313.7 1.6 multiply_convert_fusion.2
  315.9 1.4 fusion.82
  (117 shorter events, 29.9 us)
Async XLA Ops:
  7.2 176.3 %all-gather.6.cloned.1.call-start = ((), (), s32[]{:S(2)}) async-start(), calls=%async_computation.9 | async-start | bytes 4456448 | tf_op jit(solution)/shard_map/all_gather | solution.py:88
  7.9 206.9 %all-gather.4.cloned.1.call-start = ((), (), s32[]{:S(2)}) async-start(), calls=%async_computation.8 | async-start | bytes 8912896 | tf_op jit(solution)/shard_map/all_gather | solution.py:72
  50.0 55.6 %copy-start.2 = (bf16[1,128,1024]{2,1,0:T(8,128)(2,1)S(1)}, bf16[1,128,1024]{2,1,0:T(8,128)(2,1)}, u32[]{:S(2)}) copy-start(bf16[1,128,1024]{2,1,0:T(8,128)(2,1)} %param.10) | copy-start | bytes 786436
  53.1 52.4 %all-to-all-start = ((bf16[4,128,1024]{2,1,0:T(8,128)(2,1)}), bf16[4,128,1024]{2,1,0:T(8,128)(2,1)S(1)}, u32[]{:S(2)}, u32[]{:S(2)}) async-start(bf16[4,128,1024]{2,1,0:T(8,128)(2,1)} %copy.68), calls=%async_computation | async-start | bytes 2097152 | tf_op jit(solution)/shard_map/all_to_all | solution.py:17
  183.5 30.4 %copy-start.3 = (bf16[1,128,1024]{2,1,0:T(8,128)(2,1)S(1)}, bf16[1,128,1024]{2,1,0:T(8,128)(2,1)}, u32[]{:S(2)}) copy-start(bf16[1,128,1024]{2,1,0:T(8,128)(2,1)} %param.12) | copy-start | bytes 786436
  188.1 53.8 %all-to-all-start.7 = ((bf16[8,1024,32]{1,2,0:T(8,128)(2,1)}), bf16[8,1024,32]{1,2,0:T(8,128)(2,1)S(1)}, u32[]{:S(2)}, u32[]{:S(2)}) async-start(bf16[8,1024,32]{1,2,0:T(8,128)(2,1)} %bitcast.40), calls=%async_computation.7 | async-start | bytes 1048576 | tf_op jit(solution)/shard_map/all_to_all | solution.py:17
  241.9 12.5 %all-to-all-start.4 = ((bf16[128,16,64]{0,2,1:T(8,128)(2,1)}), bf16[128,16,64]{0,2,1:T(8,128)(2,1)S(1)}, u32[]{:S(2)}, u32[]{:S(2)}) async-start(bf16[128,16,64]{0,2,1:T(8,128)(2,1)} %bitcast.10), calls=%async_computation.4 | async-start | bytes 524288 | tf_op jit(solution)/shard_map/all_to_all | solution.py:79
  254.4 12.1 %all-to-all-start.5 = ((bf16[128,16,64]{0,2,1:T(8,128)(2,1)}), bf16[128,16,64]{0,2,1:T(8,128)(2,1)S(1)}, u32[]{:S(2)}, u32[]{:S(2)}) async-start(bf16[128,16,64]{0,2,1:T(8,128)(2,1)} %bitcast.14), calls=%async_computation.5 | async-start | bytes 524288 | tf_op jit(solution)/shard_map/all_to_all | solution.py:80
  268.5 3.6 %copy-start.5 = (f32[2048,64]{0,1:T(8,128)S(1)}, f32[2048,64]{0,1:T(8,128)}, u32[]{:S(2)}) copy-start(f32[2048,64]{0,1:T(8,128)} %get-tuple-element.278) | copy-start | bytes 1572868 | tf_op jit(solution)/shard_map/while
  269.3 1.9 copy-start
  272.0 3.6 %copy-start.1 = (f32[512,2048]{1,0:T(8,128)S(1)}, f32[512,2048]{1,0:T(8,128)}, u32[]{:S(2)}) copy-start(f32[512,2048]{1,0:T(8,128)} %copy-done) | copy-start | bytes 12582916 | tf_op jit(solution)/shard_map/while
  272.0 3.6 %copy-start.4 = (bf16[2048,64]{1,0:T(8,128)(2,1)S(1)}, bf16[2048,64]{1,0:T(8,128)(2,1)}, u32[]{:S(2)}) copy-start(bf16[2048,64]{1,0:T(8,128)(2,1)} %get-tuple-element.299) | copy-start | bytes 786436 | tf_op jit(solution)/shard_map/while
  275.5 1.7 copy-start.6
  281.2 3.6 %copy-start.5 = (f32[2048,64]{0,1:T(8,128)S(1)}, f32[2048,64]{0,1:T(8,128)}, u32[]{:S(2)}) copy-start(f32[2048,64]{0,1:T(8,128)} %get-tuple-element.278) | copy-start | bytes 1572868 | tf_op jit(solution)/shard_map/while
  282.0 1.9 copy-start
  284.7 3.6 %copy-start.1 = (f32[512,2048]{1,0:T(8,128)S(1)}, f32[512,2048]{1,0:T(8,128)}, u32[]{:S(2)}) copy-start(f32[512,2048]{1,0:T(8,128)} %copy-done) | copy-start | bytes 12582916 | tf_op jit(solution)/shard_map/while
  284.7 3.6 %copy-start.4 = (bf16[2048,64]{1,0:T(8,128)(2,1)S(1)}, bf16[2048,64]{1,0:T(8,128)(2,1)}, u32[]{:S(2)}) copy-start(bf16[2048,64]{1,0:T(8,128)(2,1)} %get-tuple-element.299) | copy-start | bytes 786436 | tf_op jit(solution)/shard_map/while
  288.2 1.7 copy-start.6
  293.8 3.6 %copy-start.5 = (f32[2048,64]{0,1:T(8,128)S(1)}, f32[2048,64]{0,1:T(8,128)}, u32[]{:S(2)}) copy-start(f32[2048,64]{0,1:T(8,128)} %get-tuple-element.278) | copy-start | bytes 1572868 | tf_op jit(solution)/shard_map/while
  294.6 1.9 copy-start
  297.4 3.6 %copy-start.1 = (f32[512,2048]{1,0:T(8,128)S(1)}, f32[512,2048]{1,0:T(8,128)}, u32[]{:S(2)}) copy-start(f32[512,2048]{1,0:T(8,128)} %copy-done) | copy-start | bytes 12582916 | tf_op jit(solution)/shard_map/while
  297.4 3.6 %copy-start.4 = (bf16[2048,64]{1,0:T(8,128)(2,1)S(1)}, bf16[2048,64]{1,0:T(8,128)(2,1)}, u32[]{:S(2)}) copy-start(bf16[2048,64]{1,0:T(8,128)(2,1)} %get-tuple-element.299) | copy-start | bytes 786436 | tf_op jit(solution)/shard_map/while
  300.9 1.7 copy-start.6
  306.5 3.6 %copy-start.5 = (f32[2048,64]{0,1:T(8,128)S(1)}, f32[2048,64]{0,1:T(8,128)}, u32[]{:S(2)}) copy-start(f32[2048,64]{0,1:T(8,128)} %get-tuple-element.278) | copy-start | bytes 1572868 | tf_op jit(solution)/shard_map/while
  307.3 1.9 copy-start
  310.1 3.6 %copy-start.1 = (f32[512,2048]{1,0:T(8,128)S(1)}, f32[512,2048]{1,0:T(8,128)}, u32[]{:S(2)}) copy-start(f32[512,2048]{1,0:T(8,128)} %copy-done) | copy-start | bytes 12582916 | tf_op jit(solution)/shard_map/while
  310.1 3.6 %copy-start.4 = (bf16[2048,64]{1,0:T(8,128)(2,1)S(1)}, bf16[2048,64]{1,0:T(8,128)(2,1)}, u32[]{:S(2)}) copy-start(bf16[2048,64]{1,0:T(8,128)(2,1)} %get-tuple-element.299) | copy-start | bytes 786436 | tf_op jit(solution)/shard_map/while
  313.6 1.7 copy-start.6
Sparse Core Ops, SparseCore 0:
  11.0 70.9 all-gather.5
  85.0 96.0 all-gather.3
